TPU v7x, 32 devices: a whole 2x2x4 slice. The times are simulated.
32 devices in a mesh: lev: 2 (over x), w: 16 (over z, y, core).
Axes of the slice: x: 2, y: 2, z: 4, core: 2. Of those that a mesh axis runs over, the one named last changes fastest.
Arguments:
- coef: float32 [512, 2, 96, 512], P('w', None, 'lev'), parts along dimension 2
- legendre: float32 [512, 512, 512], replicated
- gauss_weight: float32 [512], replicated
Outputs:
- output 1: float32 [96, 512, 1024], P('lev', 'w'), parts along dimension 0
- output 2: float32 [512, 2, 96, 512], P('w', None, 'lev'), parts along dimension 2
There are 2 independent parts. A program takes and returns all parts, laid end to end along the dimension named above; an argument that names none is the same for every part.
All inputs are finite; a program needn't handle non-finite values.
Results may differ from a plain program's by a relative error of at most 0.001.
Values sent between devices are 32-bit elements.
A program may use at most 2.25 GiB of HBM per device.

v0:
```python
import jax
import jax.numpy as jnp
from jax import lax
from jax.sharding import PartitionSpec as P

FULL_PREC = lax.Precision.HIGHEST


def solution(mesh):
    group_size = mesh.shape['w']

    def per_device(coef, legendre, gauss_weight):
        wave_loc = coef.shape[0]
        wave_num = wave_loc * group_size
        lat_loc = legendre.shape[2] // group_size
        dev_idx = lax.axis_index('w')
        leg_own = lax.dynamic_slice_in_dim(legendre, dev_idx * wave_loc, wave_loc, axis=0)
        wt_own = lax.dynamic_slice_in_dim(gauss_weight, dev_idx * lat_loc, lat_loc, axis=0)
        fourier = jnp.einsum('mrkl,mlj->mrkj', coef, leg_own, preferred_element_type=jnp.float32, precision=FULL_PREC)
        fourier = lax.all_to_all(fourier, 'w', 3, 0, tiled=True)
        spec = jnp.transpose(lax.complex(fourier[:, 0], fourier[:, 1]), (1, 2, 0))
        grid = jnp.fft.irfft(spec, n=2 * wave_num, axis=-1)
        square_hat = jnp.fft.rfft(grid * grid, axis=-1)[:, :, :wave_num] * wt_own[None, :, None]
        re_im = jnp.stack([jnp.real(square_hat), jnp.imag(square_hat)], axis=0)
        re_im = jnp.transpose(re_im, (3, 0, 1, 2))
        re_im = lax.all_to_all(re_im, 'w', 0, 3, tiled=True)
        spec_out = jnp.einsum('mrkj,mlj->mrkl', re_im, leg_own, preferred_element_type=jnp.float32, precision=FULL_PREC)
        return grid, spec_out

    return jax.shard_map(per_device, mesh=mesh, in_specs=(P('w', None, 'lev', None), P(None, None, None), P(None)), out_specs=(P('lev', 'w', None), P('w', None, 'lev', None)), check_vma=False)
```

profile of v0, /device:TPU:15, one launch (start us, length us, event | category | flops | bytes accessed | tf_op | source)
XLA Modules:
  0.0 895.8 jit_solution(4315613238997594031)
XLA Ops:
  0.6 27.7 %fusion.16 = f32[32,2,48,512]{3,2,1,0:T(8,128)} fusion(f32[32,2,48,512]{3,2,1,0:T(8,128)} %param.3, f32[512,512,512]{2,1,0:T(8,128)} %param.4, s32[]{:T(128)S(6)} %select_n.4), kind=kOutput, calls=%fused_computation.35 | convolution fusion | flops 9663676416 | bytes 46137348 | tf_op jit(solution)/shard_map/mrkl,mlj->mrkj/dot_general | solution.py:19
  28.3 21.3 %copy.34 = f32[32,2,48,512]{2,1,0,3:T(2,128)} copy(f32[32,2,48,512]{3,2,1,0:T(8,128)} %fusion.16) | data formatting | bytes 12582912 | tf_op jit(solution)/shard_map/mrkl,mlj->mrkj/dot_general | solution.py:19
  49.6 30.3 %reshape.26 = f32[16,1,98304]{2,1,0:T(1,128)} reshape(f32[512,32,2,48]{3,2,1,0:T(2,128)} %bitcast.170) | data formatting | bytes 12582912
  96.0 128.7 %all-to-all-done = f32[16,1,98304]{2,1,0:T(1,128)} async-done(((f32[16,1,98304]{2,1,0:T(1,128)}), f32[16,1,98304]{2,1,0:T(1,128)}, u32[]{:S(2)}, u32[]{:S(2)}) %all-to-all-start) | async-done | bytes 6291488 | tf_op jit(solution)/shard_map/all_to_all | solution.py:20
  225.2 19.4 %reduce = f32[16,98304]{1,0:T(8,128)} reduce(f32[16,1,98304]{2,1,0:T(1,128)} %all-to-all-done, f32[]{:T(128)} %broadcast.99), dimensions={1}, to_apply=%all_to_all.24.reduce_sub_computation | reduce | bytes 12582916 | tf_op jit(solution)/shard_map/all_to_all | solution.py:20
  244.6 37.8 %reshape.27 = f32[512,32,2,48]{3,2,1,0:T(2,128)} reshape(f32[16,98304]{1,0:T(8,128)} %reduce) | data formatting | bytes 12582912
  282.4 28.6 %copy.62 = f32[32,2,48,16,32]{0,3,4,2,1:T(8,128)} copy(f32[32,2,48,16,32]{2,1,0,4,3:T(2,128)} %bitcast.171) | data formatting | bytes 12582912 | tf_op jit(solution)/shard_map/all_to_all | solution.py:20
  311.0 18.9 %all_to_all.27 = f32[512,2,48,32]{0,3,2,1:T(8,128)} reshape(f32[16,32,2,48,32]{1,0,4,3,2:T(8,128)} %bitcast.169) | data formatting | bytes 12582912 | tf_op jit(solution)/shard_map/all_to_all | solution.py:20
  369.0 11.6 %copy.37 = f32[48,32,1024]{0,2,1:T(8,128)} copy(f32[48,32,1024]{2,1,0:T(8,128)} %get-tuple-element.13) | data formatting | bytes 12582912 | tf_op jit(solution)/shard_map/jit(fft) | solution.py:22
  380.6 11.6 %copy.38 = f32[48,32,1024]{0,2,1:T(8,128)} copy(f32[48,32,1024]{2,1,0:T(8,128)} %get-tuple-element.12) | data formatting | bytes 12582912 | tf_op jit(solution)/shard_map/jit(fft) | solution.py:22
  392.2 17.7 %bitcast_add_fusion = f32[48,32,128,8]{0,3,2,1:T(8,128)} fusion(f32[48,32,1024]{0,2,1:T(8,128)} %copy.38, f32[48,32,1024]{0,2,1:T(8,128)} %copy.37), kind=kLoop, calls=%fused_computation.109 | loop fusion | flops 1572864 | bytes 18874368 | tf_op jit(solution)/shard_map/jit(fft) | solution.py:22
  409.9 12.8 %copy.39 = f32[48,32,128,8]{2,3,1,0:T(8,128)} copy(f32[48,32,128,8]{0,3,2,1:T(8,128)} %bitcast_add_fusion) | data formatting | bytes 12582912 | tf_op jit(solution)/shard_map/jit(fft) | solution.py:22
  422.8 12.8 %copy.41 = f32[48,32,128,8]{2,3,1,0:T(8,128)} copy(f32[48,32,128,8]{0,3,2,1:T(8,128)} %bitcast.168) | data formatting | bytes 12582912 | tf_op jit(solution)/shard_map/jit(fft) | solution.py:22
  435.6 9.4 %fusion.24 = f32[48,32,8,128]{3,2,1,0:T(8,128)} fusion(f32[48,32,128,8]{2,3,1,0:T(8,128)} %copy.41), kind=kOutput, calls=%fused_computation.41 | convolution fusion | flops 2416001024 | bytes 12582912 | tf_op jit(solution)/shard_map/jit(fft) | solution.py:22
  444.9 12.8 %copy.40 = f32[48,32,128,8]{2,3,1,0:T(8,128)} copy(f32[48,32,128,8]{0,3,2,1:T(8,128)} %bitcast.167) | data formatting | bytes 12582912 | tf_op jit(solution)/shard_map/jit(fft) | solution.py:22
  457.7 9.9 %fusion.26 = f32[48,32,8,128]{3,2,1,0:T(8,128)} fusion(f32[48,32,128,8]{2,3,1,0:T(8,128)} %copy.40), kind=kOutput, calls=%fused_computation.43 | convolution fusion | flops 2416001024 | bytes 12582912 | tf_op jit(solution)/shard_map/jit(fft) | solution.py:22
  467.7 10.0 %fusion.9 = (f32[48,32,128,8]{2,3,1,0:T(8,128)S(1)}, f32[48,32,128,8]{2,3,1,0:T(8,128)S(1)}) fusion(f32[128,8]{0,1:T(8,128)S(1)} %get-tuple-element.14, f32[128,8]{0,1:T(8,128)S(1)} %get-tuple-element.15, f32[48,32,8,128]{3,2,1,0:T(8,128)S(1)} %copy-done.3, f32[48,32,8,128]{3,2,1,0:T(8,128)} %fusion.26, f32[48,32,128,8]{2,3,1,0:T(8,128)} %copy.39), kind=kOutput, calls=%fused_computation.19 | convolution fusion | flops 2428567552 | bytes 31465472 | tf_op jit(solution)/shard_map/jit(fft) | solution.py:22
  491.6 11.4 %fusion.128 = (f32[48,32,8,128]{3,2,1,0:T(8,128)}, f32[48,32,8,128]{3,2,1,0:T(8,128)}) fusion(f32[48,32,128,8]{2,3,1,0:T(8,128)} %fusion.12, f32[48,32,128,8]{2,3,1,0:T(8,128)S(1)} %get-tuple-element.4, f32[48,32,128,8]{2,3,1,0:T(8,128)S(1)} %fusion.64), kind=kOutput, calls=%fused_computation.135 | convolution fusion | flops 160432448 | bytes 31457280 | tf_op jit(solution)/shard_map/jit(fft) | solution.py:22
  503.0 11.6 %copy.42 = f32[48,32,8,128]{0,3,2,1:T(8,128)} copy(f32[48,32,8,128]{3,2,1,0:T(8,128)} %get-tuple-element.10) | data formatting | bytes 12582912 | tf_op jit(solution)/shard_map/mul | solution.py:23
  514.6 12.8 %copy.43 = f32[48,32,128,8]{2,3,1,0:T(8,128)} copy(f32[48,32,128,8]{0,3,2,1:T(8,128)} %bitcast.172) | data formatting | bytes 12582912 | tf_op jit(solution)/shard_map/mul | solution.py:23
  527.4 9.5 %fusion.19 = f32[48,32,8,128]{3,2,1,0:T(8,128)} fusion(f32[48,32,128,8]{2,3,1,0:T(8,128)} %copy.43), kind=kOutput, calls=%fused_computation.36 | convolution fusion | flops 2416001024 | bytes 12582912 | tf_op jit(solution)/shard_map/jit(fft) | solution.py:23
  536.9 10.0 %fusion.7 = (f32[48,32,128,8]{2,3,1,0:T(8,128)S(1)}, f32[48,32,128,8]{2,3,1,0:T(8,128)S(1)}) fusion(f32[128,8]{0,1:T(8,128)S(1)} %get-tuple-element.16, f32[128,8]{0,1:T(8,128)S(1)} %get-tuple-element.17, f32[48,32,8,128]{3,2,1,0:T(8,128)} %fusion.19, f32[48,32,8,128]{3,2,1,0:T(8,128)} %fusion.14, f32[48,32,128,8]{2,3,1,0:T(8,128)S(1)} %copy-done), kind=kOutput, calls=%fused_computation.13 | convolution fusion | flops 2428567552 | bytes 31465472 | tf_op jit(solution)/shard_map/jit(fft) | solution.py:23
  560.8 7.9 add_bitcast_fusion
  590.0 15.4 %copy.45 = f32[2,48,32,512]{1,2,0,3:T(8,128)} copy(f32[2,48,32,512]{3,2,1,0:T(8,128)} %pad_maximum_fusion) | data formatting | bytes 12582912 | tf_op jit(solution)/shard_map/stack | solution.py:24
  605.4 12.2 %bitcast_bitcast_fusion = f32[512,2,32,48]{3,2,1,0:T(8,128)} fusion(f32[2,48,32,512]{1,2,0,3:T(8,128)} %copy.45), kind=kLoop, calls=%fused_computation.136 | loop fusion | bytes 12582912
  617.6 20.9 %reshape.28 = f32[16,1,98304]{2,1,0:T(1,128)} reshape(f32[512,2,32,48]{3,2,1,0:T(8,128)} %bitcast_bitcast_fusion) | data formatting | bytes 12582912
  650.7 130.4 %all-to-all-done.1 = f32[16,1,98304]{2,1,0:T(1,128)} async-done(((f32[16,1,98304]{2,1,0:T(1,128)}), f32[16,1,98304]{2,1,0:T(1,128)}, u32[]{:S(2)}, u32[]{:S(2)}) %all-to-all-start.1) | async-done | bytes 6291488 | tf_op jit(solution)/shard_map/all_to_all | solution.py:26
  781.1 19.4 %reduce.1 = f32[16,98304]{1,0:T(8,128)} reduce(f32[16,1,98304]{2,1,0:T(1,128)} %all-to-all-done.1, f32[]{:T(128)} %broadcast.99), dimensions={1}, to_apply=%all_to_all.28.reduce_sub_computation | reduce | bytes 12582916 | tf_op jit(solution)/shard_map/all_to_all | solution.py:26
  800.5 16.9 %reshape.29 = f32[512,2,32,48]{3,2,1,0:T(8,128)} reshape(f32[16,98304]{1,0:T(8,128)} %reduce.1) | data formatting | bytes 12582912
  817.5 22.1 %copy.47 = f32[32,2,48,16,32]{4,3,2,1,0:T(8,128)} copy(f32[32,2,48,16,32]{2,4,1,0,3:T(8,128)} %bitcast.173) | data formatting | bytes 12582912 | tf_op jit(solution)/shard_map/all_to_all | solution.py:26
  839.6 18.9 %all_to_all.31 = f32[32,2,48,512]{3,2,1,0:T(8,128)} reshape(f32[32,2,48,16,32]{4,3,2,1,0:T(8,128)} %copy.47) | data formatting | bytes 12582912 | tf_op jit(solution)/shard_map/all_to_all | solution.py:26
  858.6 37.0 %fusion = f32[32,2,48,512]{3,2,1,0:T(8,128)} fusion(f32[32,2,48,512]{3,2,1,0:T(8,128)} %all_to_all.31, f32[512,512,512]{2,1,0:T(8,128)} %param.4, s32[]{:T(128)S(6)} %select_n.4), kind=kOutput, calls=%fused_computation | convolution fusion | flops 9663676416 | bytes 46137348 | tf_op jit(solution)/shard_map/mrkj,mlj->mrkl/dot_general | solution.py:27
  (36 shorter events, 117.0 us)
Async XLA Ops:
  79.9 144.8 %all-to-all-start = ((f32[16,1,98304]{2,1,0:T(1,128)}), f32[16,1,98304]{2,1,0:T(1,128)}, u32[]{:S(2)}, u32[]{:S(2)}) async-start(f32[16,1,98304]{2,1,0:T(1,128)} %reshape.26), calls=%async_computation | async-start | bytes 12582912 | tf_op jit(solution)/shard_map/all_to_all | solution.py:20
  345.1 4.6 copy-start.1
  359.1 2.9 copy-start.2
  359.1 3.8 copy-start.4
  457.7 9.9 %copy-start.3 = (f32[48,32,8,128]{3,2,1,0:T(8,128)S(1)}, f32[48,32,8,128]{3,2,1,0:T(8,128)}, u32[]{:S(2)}) copy-start(f32[48,32,8,128]{3,2,1,0:T(8,128)} %fusion.24) | copy-start | bytes 18874372
  527.4 9.5 %copy-start = (f32[48,32,128,8]{2,3,1,0:T(8,128)S(1)}, f32[48,32,128,8]{2,3,1,0:T(8,128)}, u32[]{:S(2)}) copy-start(f32[48,32,128,8]{2,3,1,0:T(8,128)} %copy.43) | copy-start | bytes 18874372
  575.7 7.1 copy-start.5
  638.5 142.6 %all-to-all-start.1 = ((f32[16,1,98304]{2,1,0:T(1,128)}), f32[16,1,98304]{2,1,0:T(1,128)}, u32[]{:S(2)}, u32[]{:S(2)}) async-start(f32[16,1,98304]{2,1,0:T(1,128)} %reshape.28), calls=%async_computation.1 | async-start | bytes 12582912 | tf_op jit(solution)/shard_map/all_to_all | solution.py:26
where the time goes:
time: 907 us; the launch traced here: 896 us
  local copies, waits for them, and re-layouts  383 us (42%)
  waiting for transfers between devices  259 us (29%)
  matrix products  168 us (19%)
  other arithmetic  72.9 us (8%)
  starting transfers between devices  12.4 us (1%)
    unnamed x20, local copies, waits for them, and re-layouts  138 us
    all_to_all x1, waiting for transfers between devices, per_device(): re_im = lax.all_to_all(re_im, 'w', 0, 3, tiled=True)  130 us
    all_to_all x1, waiting for transfers between devices, per_device(): fourier = lax.all_to_all(fourier, 'w', 3, 0, tiled=True)  129 us
    another operation x8, local copies, waits for them, and re-layouts, per_device(): grid = jnp.fft.irfft(spec, n=2 * wave_num, axis=-1)  73.7 us
    another operation x6, matrix products, per_device(): grid = jnp.fft.irfft(spec, n=2 * wave_num, axis=-1)  54.6 us
    another operation x6, matrix products, per_device(): jnp.fft.rfft(grid * grid, axis=-1)[:, :, :wave_num] * wt_own[None, :, None]  48.6 us
    all_to_all x3, local copies, waits for them, and re-layouts, per_device(): fourier = lax.all_to_all(fourier, 'w', 3, 0, tiled=True)  48 us
    all_to_all x2, local copies, waits for them, and re-layouts, per_device(): re_im = lax.all_to_all(re_im, 'w', 0, 3, tiled=True)  41.1 us
  transfers between devices with their start and end apart: 2, of which 2 were waited for; matrix products, arithmetic and copies ran while one was open for 2% of the time, Pallas kernels for 0%

commit v1 on v0

v1 whole, which is shorter than its diff:
```python
import functools

import jax
import jax.numpy as jnp
import numpy as np
from jax import lax
from jax.experimental import pallas as pl
from jax.experimental.pallas import tpu as pltpu
from jax.sharding import PartitionSpec as P

F32, BF16 = jnp.float32, jnp.bfloat16
VMEM_LIMIT = 60 * 1024 * 1024
CHUNKS = (16, 16, 16)


def split_bf16(x):
    hi = x.astype(BF16)
    return hi, (x - hi.astype(F32)).astype(BF16)


def dot3(a, b, dims):
    d = functools.partial(lax.dot_general, dimension_numbers=(dims, ((), ())), preferred_element_type=F32)
    return d(a[0], b[0]) + d(a[1], b[0]) + d(a[0], b[1])


def swap_blocks(tiles, blk):
    lane = lax.broadcasted_iota(jnp.int32, (8, 128), 1)
    outs = []
    for s in range(4):
        acc = None
        for i in range(4):
            shift = (blk * (i - s)) % 128
            t = pltpu.roll(tiles[i], shift, 1) if shift else tiles[i]
            acc = t if acc is None else jnp.where(lane >= blk * i, t, acc)
        outs.append(acc)
    return outs


def dft_matrices(wave_num, group):
    wave_loc = wave_num // group
    par, owner, idx = np.meshgrid(np.arange(2), np.arange(group), np.arange(wave_loc // 2), indexing='ij')
    m = (owner * wave_loc + 2 * idx + par).reshape(2, -1)
    t = (m[:, :, None] * np.arange(wave_num)[None, None, :]) % (2 * wave_num)
    ang = 2.0 * np.pi * t / (2 * wave_num)
    full = np.concatenate([np.cos(ang), -np.sin(ang)], axis=1).astype(np.float32)
    hi = full.astype(jnp.bfloat16)
    lo = (full - hi.astype(np.float32)).astype(jnp.bfloat16)
    return np.stack([hi, lo])


def to_grid_kernel(levels, chunks, coef_ref, leg_ref, *refs):
    outs, held = refs[:-1], refs[-1]
    i = pl.program_id(0)
    rows = 2 * levels
    a = coef_ref[0].reshape(rows, coef_ref.shape[3])
    b = leg_ref[0]
    res = dot3(split_bf16(a), split_bf16(b), ((1,), (0,)))
    m_abs = lax.axis_index('w') * pl.num_programs(0) + i
    n_lon = 2.0 * leg_ref.shape[2]
    res = res * jnp.where(m_abs == 0, 1.0 / n_lon, 2.0 / n_lon)
    for z in range(4):
        held[z, pl.ds(pl.multiple_of((i % 16) * rows, 8), rows), :] = res[:, 128 * z:128 * z + 128]

    @pl.when(i % 16 == 15)
    def _():
        half = pl.multiple_of((i // 16) * 8, 8)

        def body(pr, _):
            par, r = pr // 2, pr % 2
            k0 = 0
            for out, kc in zip(outs, chunks):
                for kg in range(kc // 4):
                    for z in range(4):
                        start = par * rows + r * levels + k0 + 4 * kg
                        tiles = [held[z, pl.ds(start + k4, 8, stride=2 * rows), :] for k4 in range(4)]
                        for s, t in enumerate(swap_blocks(tiles, 32)):
                            out[4 * z + s, kg, par, r, pl.ds(half, 8), :] = t
                k0 += kc
            return 0

        lax.fori_loop(0, 4, body, 0)


def physics_kernel(f_ref, dft_ref, wt_ref, *refs):
    grid_ref, h_ref = refs[-2:]
    halves = []
    for par in range(2):
        x = jnp.concatenate(
            [jnp.concatenate([f_ref[:, kg, par, r].reshape(-1, 128) for r in range(2)], axis=0) for kg in range(2)], axis=1)
        xt = split_bf16(x.T)
        halves.append(dot3(xt, (dft_ref[0, par], dft_ref[1, par]), ((1,), (0,))))
    g1, g2 = halves[0] + halves[1], halves[0] - halves[1]
    n_half = g1.shape[1]
    grid_ref[:, :, :n_half] = g1.reshape(8, 32, n_half)
    grid_ref[:, :, n_half:] = g2.reshape(8, 32, n_half)
    q1, q2 = g1 * g1, g2 * g2
    for par in range(2):
        q = split_bf16(q1 + q2 if par == 0 else q1 - q2)
        h = dot3((dft_ref[0, par], dft_ref[1, par]), q, ((1,), (1,))) * wt_ref[...]
        half_rows = h.shape[0] // 2
        for kg in range(2):
            for r in range(2):
                h_ref[:, kg, par, r] = h[r * half_rows:(r + 1) * half_rows, 128 * kg:128 * kg + 128].reshape(-1, 16, 128)


def to_spec_kernel(chunks, leg_ref, *refs):
    n = len(chunks)
    ins, out_ref, held = refs[:n], refs[-2], refs[-1]
    i = pl.program_id(0)
    levels = sum(chunks)
    rows = 2 * levels

    @pl.when(i % 16 == 0)
    def _():
        half = pl.multiple_of((i // 16) * 8, 8)

        def body(pr, _):
            par, r = pr // 2, pr % 2
            k0 = 0
            for src, kc in zip(ins, chunks):
                for kg in range(kc // 4):
                    for z in range(4):
                        start = par * rows + r * levels + k0 + 4 * kg
                        tiles = [src[4 * z + s, kg, par, r, pl.ds(half, 8), :] for s in range(4)]
                        for k4, t in enumerate(swap_blocks(tiles, 32)):
                            held[z, pl.ds(start + k4, 8, stride=2 * rows), :] = t
                k0 += kc
            return 0

        lax.fori_loop(0, 4, body, 0)

    a = jnp.concatenate([held[z, pl.ds(pl.multiple_of((i % 16) * rows, 8), rows), :] for z in range(4)], axis=1)
    res = dot3(split_bf16(a), split_bf16(leg_ref[0]), ((1,), (1,)))
    out_ref[0] = res.reshape(2, levels, res.shape[1])


def solution(mesh):
    group = mesh.shape['w']

    def per_device(coef, legendre, gauss_weight):
        wave_loc, _, levels, n_deg = coef.shape
        lat_rows = legendre.shape[2]
        lat_loc = lat_rows // group
        wave_num = wave_loc * group
        dev = lax.axis_index('w')
        wt = lax.dynamic_slice_in_dim(gauss_weight, dev * lat_loc, lat_loc, axis=0)
        wt = jnp.tile(wt, 8)[None, :]
        dft = jnp.asarray(dft_matrices(wave_num, group))
        params = pltpu.CompilerParams(vmem_limit_bytes=VMEM_LIMIT)

        def f_shape(kc):
            return (group, kc // 4, 2, 2, 16, 128)

        leg_spec = pl.BlockSpec((1, n_deg, lat_rows), lambda i: (lax.axis_index('w') * wave_loc + i, 0, 0))
        fs = pl.pallas_call(
            functools.partial(to_grid_kernel, levels, CHUNKS),
            grid=(wave_loc,),
            out_shape=[jax.ShapeDtypeStruct(f_shape(kc), F32) for kc in CHUNKS],
            in_specs=[pl.BlockSpec((1, 2, levels, n_deg), lambda i: (i, 0, 0, 0)), leg_spec],
            out_specs=[pl.BlockSpec(f_shape(kc), lambda i: (0,) * 6) for kc in CHUNKS],
            scratch_shapes=[pltpu.VMEM((4, 16 * 2 * levels, 128), F32)],
            compiler_params=params,
            cost_estimate=pl.CostEstimate(flops=10 ** 10, bytes_accessed=50 * 10 ** 6, transcendentals=0),
            name='to_grid',
        )(coef, legendre)

        grid_out = None
        hs = []
        k0 = 0
        for f, kc in zip(fs, CHUNKS):
            f = lax.all_to_all(f, 'w', 0, 0, tiled=True)
            base = k0 // 8
            prev = [] if grid_out is None else [grid_out]
            fspec = pl.BlockSpec((group, 2, 2, 2, 16, 128), lambda i: (0, i, 0, 0, 0, 0))
            grid_out, h = pl.pallas_call(
                physics_kernel,
                grid=(kc // 8,),
                out_shape=[jax.ShapeDtypeStruct((levels, lat_loc, 2 * wave_num), F32), jax.ShapeDtypeStruct(f.shape, F32)],
                in_specs=[fspec, pl.BlockSpec(dft.shape, lambda i: (0, 0, 0, 0)), pl.BlockSpec(wt.shape, lambda i: (0, 0))]
                + [pl.BlockSpec(memory_space=pl.ANY)] * len(prev),
                out_specs=[pl.BlockSpec((8, lat_loc, 2 * wave_num), functools.partial(lambda b, i: (b + i, 0, 0), base)), fspec],
                input_output_aliases={3: 0} if prev else {},
                compiler_params=params,
                cost_estimate=pl.CostEstimate(flops=kc * 2 * 10 ** 8, bytes_accessed=kc * 4 * 10 ** 5, transcendentals=0),
                name='physics',
            )(f, dft, wt, *prev)
            hs.append(lax.all_to_all(h, 'w', 0, 0, tiled=True))
            k0 += kc

        spec = None
        k0 = 0
        for part in (tuple(range(len(CHUNKS) - 1)), (len(CHUNKS) - 1,)):
            kcs = tuple(CHUNKS[c] for c in part)
            tot = sum(kcs)
            prev = [] if spec is None else [spec]
            spec = pl.pallas_call(
                functools.partial(to_spec_kernel, kcs),
                grid=(wave_loc,),
                out_shape=jax.ShapeDtypeStruct(coef.shape, F32),
                in_specs=[leg_spec] + [pl.BlockSpec(f_shape(kc), lambda i: (0,) * 6) for kc in kcs]
                + [pl.BlockSpec(memory_space=pl.ANY)] * len(prev),
                out_specs=pl.BlockSpec((1, 2, tot, n_deg), functools.partial(lambda b, i: (i, 0, b, 0), k0 // tot)),
                scratch_shapes=[pltpu.VMEM((4, 16 * 2 * tot, 128), F32)],
                input_output_aliases={1 + len(kcs): 0} if prev else {},
                compiler_params=params,
                cost_estimate=pl.CostEstimate(flops=10 ** 10, bytes_accessed=50 * 10 ** 6, transcendentals=0),
                name='to_spec',
            )(legendre, *[hs[c] for c in part], *prev)
            k0 += tot
        return grid_out, spec

    return jax.shard_map(per_device, mesh=mesh, in_specs=(P('w', None, 'lev', None), P(None, None, None), P(None)), out_specs=(P('lev', 'w', None), P('w', None, 'lev', None)), check_vma=False)
```

time: 907 us -> 390 us (0.43)
  local copies, waits for them, and re-layouts: 383 us -> 2.77 us
  waiting for transfers between devices: 259 us -> 82.8 us
  matrix products: 168 us -> 0 us
  blocking collectives: 0 us -> 158 us
  Pallas kernels: 0 us -> 130 us
  other arithmetic: 72.9 us -> 0 us
    all_to_all x2 -> x3, waiting for transfers between devices: 259 us -> 82.8 us  [the longest x2 50.7 us: per_device(): hs.append(lax.all_to_all(h, 'w', 0, 0, tiled=True))]
    all_to_all x0 -> x3, blocking collectives: none -> 158 us  [the longest x2 106 us: per_device(): f = lax.all_to_all(f, 'w', 0, 0, tiled=True)]
    unnamed x20 -> x6, local copies, waits for them, and re-layouts: 138 us -> 1.34 us
    pallas_call x0 -> x6, Pallas kernels: none -> 130 us  [the longest x2 72.1 us: per_device(): pl.pallas_call(functools.partial(to_spec_kernel, kcs), grid=(wave_loc,),...]
    another operation x12 -> x0, matrix products: 103 us -> none  [the longest x6 54.6 us: per_device(): grid = jnp.fft.irfft(spec, n=2 * wave_num, axis=-1)]
    another operation x11 -> x2, local copies, waits for them, and re-layouts: 103 us -> 0.67 us  [per_device(): wt = jnp.tile(wt, 8)[None, :]]
    all_to_all x5 -> x0, local copies, waits for them, and re-layouts: 89.1 us -> none  [the longest x3 48 us: per_device(): fourier = lax.all_to_all(fourier, 'w', 3, 0, tiled=True)]
    dot_general x2 -> x0, matrix products: 64.7 us -> none  [the longest x1 37 us: per_device(): jnp.einsum('mrkj,mlj->mrkl', re_im, leg_own, preferred_element_type=jnp.f...]
  transfers between devices with their start and end apart: 2 -> 3, of which waited for: 2 -> 3; matrix products, arithmetic and copies ran while one was open for 2% -> 0% of each run, Pallas kernels for 0% -> 15%
where the time goes in v1:
time: 390 us; the launch traced here: 388 us
  blocking collectives  158 us (41%)
  Pallas kernels  130 us (33%)
  waiting for transfers between devices  82.8 us (21%)
  starting transfers between devices  13.1 us (3%)
    all_to_all x2, blocking collectives, per_device(): f = lax.all_to_all(f, 'w', 0, 0, tiled=True)  106 us
    pallas_call x2, Pallas kernels, per_device(): pl.pallas_call(functools.partial(to_spec_kernel, kcs), grid=(wave_loc,),...  72.1 us
    all_to_all x1, blocking collectives, per_device(): hs.append(lax.all_to_all(h, 'w', 0, 0, tiled=True))  52.2 us
    all_to_all x2, waiting for transfers between devices, per_device(): hs.append(lax.all_to_all(h, 'w', 0, 0, tiled=True))  50.7 us
    pallas_call x1, Pallas kernels, per_device(): pl.pallas_call(functools.partial(to_grid_kernel, levels, CHUNKS), grid=(w...  36.8 us
    all_to_all x1, waiting for transfers between devices, per_device(): f = lax.all_to_all(f, 'w', 0, 0, tiled=True)  32.1 us
    pallas_call x3, Pallas kernels, per_device(): pl.pallas_call(physics_kernel, grid=(kc // 8,), out_shape=[jax.ShapeDtype...  21.3 us
    all_to_all x2, starting transfers between devices, per_device(): hs.append(lax.all_to_all(h, 'w', 0, 0, tiled=True))  8.83 us
  transfers between devices with their start and end apart: 3, of which 3 were waited for; matrix products, arithmetic and copies ran while one was open for 0% of the time, Pallas kernels for 15%

profile of v1, /device:TPU:15, one launch (start us, length us, event | category | flops | bytes accessed | tf_op | source)
XLA Modules:
  0.0 387.6 jit_solution(13682790547169792776)
XLA Ops:
  0.6 36.8 %to_grid.1 = (f32[16,4,2,2,16,128]{5,4,3,2,1,0:T(8,128)}, f32[16,4,2,2,16,128]{5,4,3,2,1,0:T(8,128)}, f32[16,4,2,2,16,128]{5,4,3,2,1,0:T(8,128)}) custom-call(f32[32,2,48,512]{3,2,1,0:T(8,128)} %coef_ref.1, f32[512,512,512]{2,1,0:T(8,128)} %leg_ref.5), custom_call_target="tpu_custom_call" | custom-call | flops 10000000000 | bytes 50000000 | tf_op jit(solution)/shard_map/to_grid/pallas_call | solution.py:155
  37.4 0.0 copy-start.2
  37.4 54.2 %all_to_all.30.f_ref = f32[16,4,2,2,16,128]{5,4,3,2,1,0:T(8,128)} all-to-all(f32[16,4,2,2,16,128]{5,4,3,2,1,0:T(8,128)} %get-tuple-element.12), channel_id=1, replica_groups=mesh['lev'=2,'w'=16] {'w'}, dimensions={0} | all-to-all | bytes 4194304 | tf_op jit(solution)/shard_map/all_to_all | solution.py:171
  91.7 0.0 copy-done.2
  91.7 51.8 %all_to_all.31.f_ref = f32[16,4,2,2,16,128]{5,4,3,2,1,0:T(8,128)} all-to-all(f32[16,4,2,2,16,128]{5,4,3,2,1,0:T(8,128)S(1)} %copy-done.2), channel_id=1, replica_groups=mesh['lev'=2,'w'=16] {'w'}, dimensions={0} | all-to-all | bytes 4194304 | tf_op jit(solution)/shard_map/all_to_all | solution.py:171
  143.4 4.2 %all-to-all-start = ((f32[16,4,2,2,16,128]{5,4,3,2,1,0:T(8,128)}), f32[16,4,2,2,16,128]{5,4,3,2,1,0:T(8,128)S(1)}, u32[]{:S(2)}, u32[]{:S(2)}) async-start(f32[16,4,2,2,16,128]{5,4,3,2,1,0:T(8,128)} %get-tuple-element.11), calls=%async_computation | async-start | bytes 4194304 | tf_op jit(solution)/shard_map/all_to_all | solution.py:171
  147.7 0.8 dynamic_slice.3
  148.4 0.7 broadcast_in_dim_tile.3.wt_ref
  149.1 7.1 %physics.3 = (f32[48,32,1024]{2,1,0:T(8,128)}, f32[16,4,2,2,16,128]{5,4,3,2,1,0:T(8,128)}) custom-call(f32[16,4,2,2,16,128]{5,4,3,2,1,0:T(8,128)} %all_to_all.31.f_ref, bf16[2,2,512,512]{3,2,1,0:T(8,128)(2,1)} %constant.12.clone.dft_ref, f32[1,256]{1,0:T(1,128)} %broadcast_in_dim_tile.3.wt_ref), custom_call_target="tpu_custom_call" | custom-call | flops 3200000000 | bytes 6400000 | tf_op jit(solution)/shard_map/physics/pallas_call | solution.py:175
  156.2 7.1 %physics.4 = (f32[48,32,1024]{2,1,0:T(8,128)}, f32[16,4,2,2,16,128]{5,4,3,2,1,0:T(8,128)}) custom-call(f32[16,4,2,2,16,128]{5,4,3,2,1,0:T(8,128)} %all_to_all.30.f_ref, bf16[2,2,512,512]{3,2,1,0:T(8,128)(2,1)} %constant.12.clone.dft_ref, f32[1,256]{1,0:T(1,128)} %broadcast_in_dim_tile.3.wt_ref, ...), custom_call_target="tpu_custom_call", output_to_operand_aliasing={{0}: (3, {})} | custom-call | flops 3200000000 | bytes 6400000 | tf_op jit(solution)/shard_map/physics/pallas_call | solution.py:175
  163.3 32.1 %all-to-all-done.f_ref = f32[16,4,2,2,16,128]{5,4,3,2,1,0:T(8,128)S(1)} async-done(((f32[16,4,2,2,16,128]{5,4,3,2,1,0:T(8,128)}), f32[16,4,2,2,16,128]{5,4,3,2,1,0:T(8,128)S(1)}, u32[]{:S(2)}, u32[]{:S(2)}) %all-to-all-start) | async-done | bytes 2097184 | tf_op jit(solution)/shard_map/all_to_all | solution.py:171
  195.4 0.0 copy-start.1
  195.4 52.2 %all_to_all.32.refs_1_ = f32[16,4,2,2,16,128]{5,4,3,2,1,0:T(8,128)} all-to-all(f32[16,4,2,2,16,128]{5,4,3,2,1,0:T(8,128)} %get-tuple-element.19), channel_id=1, replica_groups=mesh['lev'=2,'w'=16] {'w'}, dimensions={0} | all-to-all | bytes 4194304 | tf_op jit(solution)/shard_map/all_to_all | solution.py:187
  247.6 0.0 copy-done.1
  247.6 4.2 %all-to-all-start.4 = ((f32[16,4,2,2,16,128]{5,4,3,2,1,0:T(8,128)}), f32[16,4,2,2,16,128]{5,4,3,2,1,0:T(8,128)S(1)}, u32[]{:S(2)}, u32[]{:S(2)}) async-start(f32[16,4,2,2,16,128]{5,4,3,2,1,0:T(8,128)} %get-tuple-element.18), calls=%async_computation.4 | async-start | bytes 4194304 | tf_op jit(solution)/shard_map/all_to_all | solution.py:187
  251.8 7.1 %physics.5 = (f32[48,32,1024]{2,1,0:T(8,128)}, f32[16,4,2,2,16,128]{5,4,3,2,1,0:T(8,128)}) custom-call(f32[16,4,2,2,16,128]{5,4,3,2,1,0:T(8,128)} %copy-done.1, bf16[2,2,512,512]{3,2,1,0:T(8,128)(2,1)} %constant.12.clone.dft_ref, f32[1,256]{1,0:T(1,128)} %broadcast_in_dim_tile.3.wt_ref, ...), custom_call_target="tpu_custom_call", output_to_operand_aliasing={{0}: (3, {})} | custom-call | flops 3200000000 | bytes 6400000 | tf_op jit(solution)/shard_map/physics/pallas_call | solution.py:175
  258.9 40.6 %all-to-all-done.4.refs_0_ = f32[16,4,2,2,16,128]{5,4,3,2,1,0:T(8,128)S(1)} async-done(((f32[16,4,2,2,16,128]{5,4,3,2,1,0:T(8,128)}), f32[16,4,2,2,16,128]{5,4,3,2,1,0:T(8,128)S(1)}, u32[]{:S(2)}, u32[]{:S(2)}) %all-to-all-start.4) | async-done | bytes 2097184 | tf_op jit(solution)/shard_map/all_to_all | solution.py:187
  299.6 0.0 copy-start
  299.6 1.3 copy-done
  300.9 4.6 %all-to-all-start.3 = ((f32[16,4,2,2,16,128]{5,4,3,2,1,0:T(8,128)}), f32[16,4,2,2,16,128]{5,4,3,2,1,0:T(8,128)}, u32[]{:S(2)}, u32[]{:S(2)}) async-start(f32[16,4,2,2,16,128]{5,4,3,2,1,0:T(8,128)} %get-tuple-element.17), calls=%async_computation.3 | async-start | bytes 4194304 | tf_op jit(solution)/shard_map/all_to_all | solution.py:187
  305.5 37.7 %to_spec.2.refs_1_ = f32[32,2,48,512]{3,2,1,0:T(8,128)} custom-call(f32[512,512,512]{2,1,0:T(8,128)} %leg_ref.5, f32[16,4,2,2,16,128]{5,4,3,2,1,0:T(8,128)} %copy-done, f32[16,4,2,2,16,128]{5,4,3,2,1,0:T(8,128)} %all_to_all.32.refs_1_), custom_call_target="tpu_custom_call" | custom-call | flops 10000000000 | bytes 50000000 | tf_op jit(solution)/shard_map/to_spec/pallas_call | solution.py:196
  343.2 10.0 %all-to-all-done.3.refs_0_ = f32[16,4,2,2,16,128]{5,4,3,2,1,0:T(8,128)} async-done(((f32[16,4,2,2,16,128]{5,4,3,2,1,0:T(8,128)}), f32[16,4,2,2,16,128]{5,4,3,2,1,0:T(8,128)}, u32[]{:S(2)}, u32[]{:S(2)}) %all-to-all-start.3) | async-done | bytes 2097184 | tf_op jit(solution)/shard_map/all_to_all | solution.py:187
  353.2 34.3 %to_spec.3 = f32[32,2,48,512]{3,2,1,0:T(8,128)} custom-call(f32[512,512,512]{2,1,0:T(8,128)} %leg_ref.5, f32[16,4,2,2,16,128]{5,4,3,2,1,0:T(8,128)} %all-to-all-done.3.refs_0_, f32[32,2,48,512]{3,2,1,0:T(8,128)} %to_spec.2.refs_1_), custom_call_target="tpu_custom_call", output_to_operand_aliasing={{}: (2, {})} | custom-call | flops 10000000000 | bytes 50000000 | tf_op jit(solution)/shard_map/to_spec/pallas_call | solution.py:196
  (1 shorter events, 0.0 us)
Async XLA Ops:
  37.4 54.2 %copy-start.2 = (f32[16,4,2,2,16,128]{5,4,3,2,1,0:T(8,128)S(1)}, f32[16,4,2,2,16,128]{5,4,3,2,1,0:T(8,128)}, u32[]{:S(2)}) copy-start(f32[16,4,2,2,16,128]{5,4,3,2,1,0:T(8,128)} %get-tuple-element.13) | copy-start | bytes 6291460
  143.4 52.0 %all-to-all-start = ((f32[16,4,2,2,16,128]{5,4,3,2,1,0:T(8,128)}), f32[16,4,2,2,16,128]{5,4,3,2,1,0:T(8,128)S(1)}, u32[]{:S(2)}, u32[]{:S(2)}) async-start(f32[16,4,2,2,16,128]{5,4,3,2,1,0:T(8,128)} %get-tuple-element.11), calls=%async_computation | async-start | bytes 4194304 | tf_op jit(solution)/shard_map/all_to_all | solution.py:171
  195.4 52.2 %copy-start.1 = (f32[16,4,2,2,16,128]{5,4,3,2,1,0:T(8,128)}, f32[16,4,2,2,16,128]{5,4,3,2,1,0:T(8,128)S(1)}, u32[]{:S(2)}) copy-start(f32[16,4,2,2,16,128]{5,4,3,2,1,0:T(8,128)S(1)} %all-to-all-done.f_ref) | copy-start | bytes 6291460
  247.6 52.0 %all-to-all-start.4 = ((f32[16,4,2,2,16,128]{5,4,3,2,1,0:T(8,128)}), f32[16,4,2,2,16,128]{5,4,3,2,1,0:T(8,128)S(1)}, u32[]{:S(2)}, u32[]{:S(2)}) async-start(f32[16,4,2,2,16,128]{5,4,3,2,1,0:T(8,128)} %get-tuple-element.18), calls=%async_computation.4 | async-start | bytes 4194304 | tf_op jit(solution)/shard_map/all_to_all | solution.py:187
  299.6 1.3 copy-start
  300.9 52.3 %all-to-all-start.3 = ((f32[16,4,2,2,16,128]{5,4,3,2,1,0:T(8,128)}), f32[16,4,2,2,16,128]{5,4,3,2,1,0:T(8,128)}, u32[]{:S(2)}, u32[]{:S(2)}) async-start(f32[16,4,2,2,16,128]{5,4,3,2,1,0:T(8,128)} %get-tuple-element.17), calls=%async_computation.3 | async-start | bytes 4194304 | tf_op jit(solution)/shard_map/all_to_all | solution.py:187

commit v2 on v0

v2 whole, which is shorter than its diff:
```python
import functools

import jax
import jax.numpy as jnp
import numpy as np
from jax import lax
from jax.experimental import pallas as pl
from jax.experimental.pallas import tpu as pltpu
from jax.sharding import PartitionSpec as P

F32, BF16 = jnp.float32, jnp.bfloat16
VMEM_LIMIT = 63 * 1024 * 1024
RING = 4


def split_bf16(x):
    hi = x.astype(BF16)
    return hi, (x - hi.astype(F32)).astype(BF16)


def dot3(a, b, dims):
    d = functools.partial(lax.dot_general, dimension_numbers=(dims, ((), ())), preferred_element_type=F32)
    return d(a[0], b[0]) + d(a[1], b[0]) + d(a[0], b[1])


def swap_blocks(tiles, blk):
    lane = lax.broadcasted_iota(jnp.int32, (8, 128), 1)
    outs = []
    for s in range(4):
        acc = None
        for i in range(4):
            shift = (blk * (i - s)) % 128
            t = pltpu.roll(tiles[i], shift, 1) if shift else tiles[i]
            acc = t if acc is None else jnp.where(lane >= blk * i, t, acc)
        outs.append(acc)
    return outs


def dft_matrices(wave_num, group):
    wave_loc = wave_num // group
    par, owner, idx = np.meshgrid(np.arange(2), np.arange(group), np.arange(wave_loc // 2), indexing='ij')
    m = (owner * wave_loc + 2 * idx + par).reshape(2, -1)
    t = (m[:, :, None] * np.arange(wave_num)[None, None, :]) % (2 * wave_num)
    ang = 2.0 * np.pi * t / (2 * wave_num)
    full = np.concatenate([np.cos(ang), -np.sin(ang)], axis=1).astype(np.float32)
    hi = full.astype(jnp.bfloat16)
    lo = (full - hi.astype(np.float32)).astype(jnp.bfloat16)
    return np.stack([hi, lo])


def whole_kernel(group, coef, leg, dft_hbm, wt_ref, grid_out, spec_out,
                 f_send, x_recv, h_send, y_recv, held, leg_buf, coef_buf, dft, stage, spec_buf,
                 leg_sem, coef_sem, dft_sem, stage_sem, spec_sem, f_ssem, h_ssem, x_sem, y_sem):
    wave_loc, _, levels, n_deg = coef.shape
    rows = 2 * levels
    n_kg = levels // 4
    n_chunk = levels // 8
    lev, me = lax.axis_index('lev'), lax.axis_index('w')

    def peer(j):
        return lax.rem(me + j, group)

    barrier = pltpu.get_barrier_semaphore()

    def greet(j, _):
        pl.semaphore_signal(barrier, inc=1, device_id=(lev, peer(j)), device_id_type=pl.DeviceIdType.MESH)
        return 0

    lax.fori_loop(1, group, greet, 0)

    def wave_of(t):
        q, mm = t // 8, t % 8
        return 16 * (q // 2) + 2 * mm + q % 2

    def leg_copy(t):
        return pltpu.make_async_copy(leg.at[me * wave_loc + wave_of(t)], leg_buf.at[t % RING], leg_sem.at[t % RING])

    def coef_copy(t):
        return pltpu.make_async_copy(coef.at[wave_of(t)], coef_buf.at[t % RING], coef_sem.at[t % RING])

    def dft_copy():
        return pltpu.make_async_copy(dft_hbm, dft, dft_sem)

    def stage_copy(c):
        return pltpu.make_async_copy(stage.at[c % 2], grid_out.at[pl.ds(c * 8, 8)], stage_sem.at[c % 2])

    def spec_copy(t):
        return pltpu.make_async_copy(spec_buf.at[t % 2], spec_out.at[wave_of(t)], spec_sem.at[t % 2])

    def remote(src, dst, ssem, rsem, j):
        pltpu.make_async_remote_copy(src, dst, ssem, rsem, device_id=(lev, peer(j)), device_id_type=pl.DeviceIdType.MESH).start()

    for t in range(RING):
        leg_copy(t).start()
        coef_copy(t).start()
    dft_copy().start()

    for q in range(4):
        half, par = q // 2, q % 2

        def wave_in(mm, _):
            t = q * 8 + mm
            coef_copy(t).wait()
            leg_copy(t).wait()
            a = split_bf16(coef_buf[t % RING].reshape(rows, n_deg))
            res = dot3(a, split_bf16(leg_buf[t % RING]), ((1,), (0,)))
            m_abs = me * wave_loc + wave_of(t)
            n_lon = 2.0 * wave_loc * group
            res = res * jnp.where(m_abs == 0, 1.0 / n_lon, 2.0 / n_lon)
            for z in range(4):
                held[z, pl.ds(pl.multiple_of(mm * rows, 8), rows), :] = res[:, 128 * z:128 * z + 128]

            @pl.when(t + RING < wave_loc)
            def _():
                leg_copy(t + RING).start()
                coef_copy(t + RING).start()

            return 0

        lax.fori_loop(0, 8, wave_in, 0)

        def scatter(kr, _):
            kg, r = kr // 2, kr % 2
            for z in range(4):
                tiles = [held[z, pl.ds(r * levels + 4 * kg + k4, 8, stride=rows), :] for k4 in range(4)]
                for s, tile in enumerate(swap_blocks(tiles, 32)):
                    f_send[q, 4 * z + s, kg, r] = tile
            return 0

        lax.fori_loop(0, 2 * n_kg, scatter, 0)
        if q == 0:
            pl.semaphore_wait(barrier, group - 1)
        if q < 3:
            def send(j, _):
                remote(f_send.at[q, peer(j)], x_recv.at[:, par, :, me, half], f_ssem.at[q], x_sem.at[q], j)
                return 0

            lax.fori_loop(1, group, send, 0)
        else:
            def send(n, _):
                c, j = n // (group - 1), n % (group - 1) + 1
                remote(f_send.at[q, peer(j), pl.ds(2 * c, 2)], x_recv.at[pl.ds(2 * c, 2), par, :, me, half], f_ssem.at[q], x_sem.at[3 + c], j)
                return 0

            lax.fori_loop(0, n_chunk * (group - 1), send, 0)

        def keep(kg, _):
            x_recv[kg, par, :, me, half] = f_send[q, me, kg]
            return 0

        lax.fori_loop(0, n_kg, keep, 0)

    for t in range(RING):
        leg_copy(t).start()
    dft_copy().wait()
    for q in range(3):
        half, par = q // 2, q % 2
        blk = x_recv.at[:, par, :, pl.ds(0, group - 1), half]
        pltpu.make_async_copy(blk, blk, x_sem.at[q]).wait()

    def physics(c, _):
        blk = x_recv.at[pl.ds(2 * c, 2), 1, :, pl.ds(0, group - 1), 1]
        pltpu.make_async_copy(blk, blk, x_sem.at[3 + c]).wait()
        halves = []
        for par in range(2):
            x = jnp.concatenate(
                [jnp.concatenate([x_recv[2 * c + kg, par, r].reshape(-1, 128) for r in range(2)], axis=0) for kg in range(2)], axis=1)
            halves.append(dot3(split_bf16(x.T), (dft[0, par], dft[1, par]), ((1,), (0,))))
        g1, g2 = halves[0] + halves[1], halves[0] - halves[1]
        n_half = g1.shape[1]

        @pl.when(c >= 2)
        def _():
            stage_copy(c - 2).wait()

        stage[c % 2, :, :, :n_half] = g1.reshape(8, -1, n_half)
        stage[c % 2, :, :, n_half:] = g2.reshape(8, -1, n_half)
        stage_copy(c).start()
        q1, q2 = g1 * g1, g2 * g2
        for par in range(2):
            qs = split_bf16(q1 + q2 if par == 0 else q1 - q2)
            h = dot3((dft[0, par], dft[1, par]), qs, ((1,), (1,))) * wt_ref[...]
            half_rows = h.shape[0] // 2
            for kg in range(2):
                for r in range(2):
                    blk = h[r * half_rows:(r + 1) * half_rows, 128 * kg:128 * kg + 128].reshape(group, 2, 8, 128)
                    for half in range(2):
                        h_send[2 * half + par, :, 2 * c + kg, r] = blk[:, half]

        def send(n, _):
            q, j = n // (group - 1), n % (group - 1) + 1
            ks = pl.ds(2 * c, 2)
            remote(h_send.at[q, peer(j), ks], y_recv.at[q, me, ks], h_ssem.at[q], y_sem.at[q], j)
            return 0

        lax.fori_loop(0, 2 * (group - 1), send, 0)
        return 0

    lax.fori_loop(0, n_chunk, physics, 0)
    for q in range(2, 4):
        def send(j, _):
            remote(h_send.at[q, peer(j)], y_recv.at[q, me], h_ssem.at[q], y_sem.at[q], j)
            return 0

        lax.fori_loop(1, group, send, 0)

    for q in range(4):
        def keep(kg, _):
            y_recv[q, me, kg] = h_send[q, me, kg]
            return 0

        lax.fori_loop(0, n_kg, keep, 0)
        blk = y_recv.at[q, pl.ds(0, group - 1)]
        pltpu.make_async_copy(blk, blk, y_sem.at[q]).wait()

        def gather(kr, _):
            kg, r = kr // 2, kr % 2
            for z in range(4):
                tiles = [y_recv[q, 4 * z + s, kg, r] for s in range(4)]
                for k4, tile in enumerate(swap_blocks(tiles, 32)):
                    held[z, pl.ds(r * levels + 4 * kg + k4, 8, stride=rows), :] = tile
            return 0

        lax.fori_loop(0, 2 * n_kg, gather, 0)

        def wave_out(mm, _):
            t = q * 8 + mm
            a = jnp.concatenate([held[z, pl.ds(pl.multiple_of(mm * rows, 8), rows), :] for z in range(4)], axis=1)
            leg_copy(t).wait()
            res = dot3(split_bf16(a), split_bf16(leg_buf[t % RING]), ((1,), (1,)))

            @pl.when(t + RING < wave_loc)
            def _():
                leg_copy(t + RING).start()

            @pl.when(t >= 2)
            def _():
                spec_copy(t - 2).wait()

            spec_buf[t % 2] = res.reshape(2, levels, n_deg)
            spec_copy(t).start()
            return 0

        lax.fori_loop(0, 8, wave_out, 0)

    spec_copy(wave_loc - 2).wait()
    spec_copy(wave_loc - 1).wait()
    stage_copy(n_chunk - 2).wait()
    stage_copy(n_chunk - 1).wait()
    for q in range(4):
        blk = f_send.at[q, pl.ds(0, group - 1)]
        pltpu.make_async_copy(blk, blk, f_ssem.at[q]).wait()
        blk = h_send.at[q, pl.ds(0, group - 1)]
        pltpu.make_async_copy(blk, blk, h_ssem.at[q]).wait()


def solution(mesh):
    group = mesh.shape['w']

    def per_device(coef, legendre, gauss_weight):
        wave_loc, _, levels, n_deg = coef.shape
        lat_rows = legendre.shape[2]
        lat_loc = lat_rows // group
        wave_num = wave_loc * group
        n_kg = levels // 4
        dev = lax.axis_index('w')
        wt = lax.dynamic_slice_in_dim(gauss_weight, dev * lat_loc, lat_loc, axis=0)
        wt = jnp.tile(wt, 8)[None, :]
        dft = jnp.asarray(dft_matrices(wave_num, group))
        hbm = pl.BlockSpec(memory_space=pl.ANY)
        dma = pltpu.SemaphoreType.DMA
        return pl.pallas_call(
            functools.partial(whole_kernel, group),
            out_shape=[jax.ShapeDtypeStruct((levels, lat_loc, 2 * wave_num), F32), jax.ShapeDtypeStruct(coef.shape, F32)],
            in_specs=[hbm, hbm, hbm, pl.BlockSpec(memory_space=pltpu.VMEM)],
            out_specs=[hbm, hbm],
            scratch_shapes=[
                pltpu.VMEM((4, group, n_kg, 2, 8, 128), F32),
                pltpu.VMEM((n_kg, 2, 2, group, 2, 8, 128), F32),
                pltpu.VMEM((4, group, n_kg, 2, 8, 128), F32),
                pltpu.VMEM((4, group, n_kg, 2, 8, 128), F32),
                pltpu.VMEM((4, 8 * 2 * levels, 128), F32),
                pltpu.VMEM((RING, n_deg, lat_rows), F32),
                pltpu.VMEM((RING, 2, levels, n_deg), F32),
                pltpu.VMEM(dft.shape, BF16),
                pltpu.VMEM((2, 8, lat_loc, 2 * wave_num), F32),
                pltpu.VMEM((2, 2, levels, n_deg), F32),
                dma((RING,)), dma((RING,)), dma, dma((2,)), dma((2,)), dma((4,)), dma((4,)), dma((3 + levels // 8,)), dma((4,)),
            ],
            compiler_params=pltpu.CompilerParams(vmem_limit_bytes=VMEM_LIMIT, collective_id=0, has_side_effects=True),
            name='transform_pair',
        )(coef, legendre, dft, wt)

    return jax.shard_map(per_device, mesh=mesh, in_specs=(P('w', None, 'lev', None), P(None, None, None), P(None)), out_specs=(P('lev', 'w', None), P('w', None, 'lev', None)), check_vma=False)
```

time: 907 us -> 305 us (0.34)
  local copies, waits for them, and re-layouts: 383 us -> 10.9 us
  Pallas kernels: 0 us -> 291 us
  waiting for transfers between devices: 259 us -> 0 us
  matrix products: 168 us -> 0 us
  other arithmetic: 72.9 us -> 0 us
  starting transfers between devices: 12.4 us -> 0 us
    pallas_call x0 -> x1, Pallas kernels: none -> 291 us  [per_device(): pl.pallas_call(functools.partial(whole_kernel, group), out_shape=[jax.Sha...]
    all_to_all x2 -> x0, waiting for transfers between devices: 259 us -> none  [the longest x1 130 us: per_device(): re_im = lax.all_to_all(re_im, 'w', 0, 3, tiled=True)]
    unnamed x20 -> x4, local copies, waits for them, and re-layouts: 138 us -> 9.47 us
    another operation x12 -> x0, matrix products: 103 us -> none  [the longest x6 54.6 us: per_device(): grid = jnp.fft.irfft(spec, n=2 * wave_num, axis=-1)]
    another operation x11 -> x2, local copies, waits for them, and re-layouts: 103 us -> 0.65 us  [per_device(): wt = jnp.tile(wt, 8)[None, :]]
    all_to_all x5 -> x0, local copies, waits for them, and re-layouts: 89.1 us -> none  [the longest x3 48 us: per_device(): fourier = lax.all_to_all(fourier, 'w', 3, 0, tiled=True)]
    dot_general x2 -> x0, matrix products: 64.7 us -> none  [the longest x1 37 us: per_device(): jnp.einsum('mrkj,mlj->mrkl', re_im, leg_own, preferred_element_type=jnp.f...]
    all_to_all x2 -> x0, other arithmetic: 38.8 us -> none  [the longest x1 19.4 us: per_device(): re_im = lax.all_to_all(re_im, 'w', 0, 3, tiled=True)]
  transfers between devices with their start and end apart: 2 -> 0, of which waited for: 2 -> 0; matrix products, arithmetic and copies ran while one was open for 2% -> 0% of each run, Pallas kernels for 0% -> 0%
where the time goes in v2:
time: 305 us; the launch traced here: 302 us
  Pallas kernels  291 us (95%)
  local copies, waits for them, and re-layouts  10.9 us (4%)
    pallas_call x1, Pallas kernels, per_device(): pl.pallas_call(functools.partial(whole_kernel, group), out_shape=[jax.Sha...  291 us
    unnamed x4, local copies, waits for them, and re-layouts  9.47 us

profile of v2, /device:TPU:15, one launch (start us, length us, event | category | flops | bytes accessed | tf_op | source)
XLA Modules:
  0.0 302.4 jit_solution(917895201524569166)
XLA Ops:
  0.6 0.8 dynamic_slice.3
  1.4 0.6 broadcast_in_dim_tile.3.wt_ref
  2.0 290.9 %transform_pair.1 = (f32[48,32,1024]{2,1,0:T(8,128)}, f32[32,2,48,512]{3,2,1,0:T(8,128)}) custom-call(f32[32,2,48,512]{3,2,1,0:T(8,128)} %coef.1, f32[512,512,512]{2,1,0:T(8,128)} %leg.1, bf16[2,2,512,512]{3,2,1,0:T(8,128)(2,1)} %constant.12.clone.dft_hbm, f32[1,256]{1,0:T(1,128)} %broadcast_in_dim_tile.3.wt_ref), custom_call_target="tpu_custom_call" | custom-call | tf_op jit(solution)/shard_map/transform_pair/pallas_call | solution.py:272
  292.9 0.0 copy-start
  292.9 6.8 %copy.8 = f32[48,32,1024]{2,1,0:T(8,128)} copy(f32[48,32,1024]{2,1,0:T(8,128)} %get-tuple-element.4) | data formatting | bytes 12582912
  299.7 0.0 copy-done
  299.7 2.7 copy.9
  (1 shorter events, 0.0 us)
Async XLA Ops:
  292.9 6.8 %copy-start = (f32[32,2,48,512]{3,2,1,0:T(8,128)S(1)}, f32[32,2,48,512]{3,2,1,0:T(8,128)}, u32[]{:S(2)}) copy-start(f32[32,2,48,512]{3,2,1,0:T(8,128)} %get-tuple-element.5) | copy-start | bytes 18874372

commit v3 on v2

--- a/solution.py
+++ b/solution.py
@@ -9,7 +9,7 @@
 from jax.sharding import PartitionSpec as P
 
 F32, BF16 = jnp.float32, jnp.bfloat16
-VMEM_LIMIT = 63 * 1024 * 1024
+VMEM_LIMIT = 50 * 1024 * 1024
 RING = 4
 
 
@@ -36,6 +36,13 @@
     return outs
 
 
+def dot3_stacked(a, b, dims):
+    d = functools.partial(lax.dot_general, dimension_numbers=(dims, ((), ())), preferred_element_type=F32)
+    n = a[0].shape[0]
+    both = d(jnp.concatenate(a, axis=0), b[0])
+    return both[:n] + both[n:] + d(a[0], b[1])
+
+
 def dft_matrices(wave_num, group):
     wave_loc = wave_num // group
     par, owner, idx = np.meshgrid(np.arange(2), np.arange(group), np.arange(wave_loc // 2), indexing='ij')
@@ -49,8 +56,8 @@
 
 
 def whole_kernel(group, coef, leg, dft_hbm, wt_ref, grid_out, spec_out,
-                 f_send, x_recv, h_send, y_recv, held, leg_buf, coef_buf, dft, stage, spec_buf,
-                 leg_sem, coef_sem, dft_sem, stage_sem, spec_sem, f_ssem, h_ssem, x_sem, y_sem):
+                 f_send, x_recv, h_send, y_recv, held, leg_buf, coef_buf, dft,
+                 leg_sem, coef_sem, dft_sem, f_ssem, h_ssem, x_sem, y_sem):
     wave_loc, _, levels, n_deg = coef.shape
     rows = 2 * levels
     n_kg = levels // 4
@@ -81,12 +88,6 @@
     def dft_copy():
         return pltpu.make_async_copy(dft_hbm, dft, dft_sem)
 
-    def stage_copy(c):
-        return pltpu.make_async_copy(stage.at[c % 2], grid_out.at[pl.ds(c * 8, 8)], stage_sem.at[c % 2])
-
-    def spec_copy(t):
-        return pltpu.make_async_copy(spec_buf.at[t % 2], spec_out.at[wave_of(t)], spec_sem.at[t % 2])
-
     def remote(src, dst, ssem, rsem, j):
         pltpu.make_async_remote_copy(src, dst, ssem, rsem, device_id=(lev, peer(j)), device_id_type=pl.DeviceIdType.MESH).start()
 
@@ -94,6 +95,13 @@
         leg_copy(t).start()
         coef_copy(t).start()
     dft_copy().start()
+
+    lane = lax.broadcasted_iota(jnp.int32, (1, 128), 1)
+    wt = pltpu.roll(wt_ref[pl.ds(me // 4, 1), :], lax.rem(128 - 32 * lax.rem(me, 4), 128), 1)
+    wt = jnp.where(lane < 32, wt, 0.0)
+    wt = wt + pltpu.roll(wt, 32, 1)
+    wt = wt + pltpu.roll(wt, 64, 1)
+    wt = jnp.concatenate([wt, wt], axis=1)
 
     for q in range(4):
         half, par = q // 2, q % 2
@@ -103,7 +111,7 @@
             coef_copy(t).wait()
             leg_copy(t).wait()
             a = split_bf16(coef_buf[t % RING].reshape(rows, n_deg))
-            res = dot3(a, split_bf16(leg_buf[t % RING]), ((1,), (0,)))
+            res = dot3_stacked(a, split_bf16(leg_buf[t % RING]), ((1,), (0,)))
             m_abs = me * wave_loc + wave_of(t)
             n_lon = 2.0 * wave_loc * group
             res = res * jnp.where(m_abs == 0, 1.0 / n_lon, 2.0 / n_lon)
@@ -169,17 +177,12 @@
         g1, g2 = halves[0] + halves[1], halves[0] - halves[1]
         n_half = g1.shape[1]
 
-        @pl.when(c >= 2)
-        def _():
-            stage_copy(c - 2).wait()
-
-        stage[c % 2, :, :, :n_half] = g1.reshape(8, -1, n_half)
-        stage[c % 2, :, :, n_half:] = g2.reshape(8, -1, n_half)
-        stage_copy(c).start()
+        grid_out[pl.ds(c * 8, 8), :, :n_half] = g1.reshape(8, -1, n_half)
+        grid_out[pl.ds(c * 8, 8), :, n_half:] = g2.reshape(8, -1, n_half)
         q1, q2 = g1 * g1, g2 * g2
         for par in range(2):
             qs = split_bf16(q1 + q2 if par == 0 else q1 - q2)
-            h = dot3((dft[0, par], dft[1, par]), qs, ((1,), (1,))) * wt_ref[...]
+            h = dot3((dft[0, par], dft[1, par]), qs, ((1,), (1,))) * wt
             half_rows = h.shape[0] // 2
             for kg in range(2):
                 for r in range(2):
@@ -197,12 +200,14 @@
         return 0
 
     lax.fori_loop(0, n_chunk, physics, 0)
-    for q in range(2, 4):
+    def send_h(q):
         def send(j, _):
             remote(h_send.at[q, peer(j)], y_recv.at[q, me], h_ssem.at[q], y_sem.at[q], j)
             return 0
 
         lax.fori_loop(1, group, send, 0)
+
+    send_h(2)
 
     for q in range(4):
         def keep(kg, _):
@@ -227,26 +232,19 @@
             t = q * 8 + mm
             a = jnp.concatenate([held[z, pl.ds(pl.multiple_of(mm * rows, 8), rows), :] for z in range(4)], axis=1)
             leg_copy(t).wait()
-            res = dot3(split_bf16(a), split_bf16(leg_buf[t % RING]), ((1,), (1,)))
+            res = dot3_stacked(split_bf16(a), split_bf16(leg_buf[t % RING]), ((1,), (1,)))
 
             @pl.when(t + RING < wave_loc)
             def _():
                 leg_copy(t + RING).start()
 
-            @pl.when(t >= 2)
-            def _():
-                spec_copy(t - 2).wait()
-
-            spec_buf[t % 2] = res.reshape(2, levels, n_deg)
-            spec_copy(t).start()
+            spec_out[wave_of(t)] = res.reshape(2, levels, n_deg)
             return 0
 
         lax.fori_loop(0, 8, wave_out, 0)
-
-    spec_copy(wave_loc - 2).wait()
-    spec_copy(wave_loc - 1).wait()
-    stage_copy(n_chunk - 2).wait()
-    stage_copy(n_chunk - 1).wait()
+        if q == 1:
+            send_h(3)
+
     for q in range(4):
         blk = f_send.at[q, pl.ds(0, group - 1)]
         pltpu.make_async_copy(blk, blk, f_ssem.at[q]).wait()
@@ -263,17 +261,15 @@
         lat_loc = lat_rows // group
         wave_num = wave_loc * group
         n_kg = levels // 4
-        dev = lax.axis_index('w')
-        wt = lax.dynamic_slice_in_dim(gauss_weight, dev * lat_loc, lat_loc, axis=0)
-        wt = jnp.tile(wt, 8)[None, :]
+        wt = gauss_weight.reshape(4, 128)
         dft = jnp.asarray(dft_matrices(wave_num, group))
         hbm = pl.BlockSpec(memory_space=pl.ANY)
         dma = pltpu.SemaphoreType.DMA
         return pl.pallas_call(
             functools.partial(whole_kernel, group),
-            out_shape=[jax.ShapeDtypeStruct((levels, lat_loc, 2 * wave_num), F32), jax.ShapeDtypeStruct(coef.shape, F32)],
+            out_shape=[pltpu.VMEM((levels, lat_loc, 2 * wave_num), F32), pltpu.VMEM(coef.shape, F32)],
             in_specs=[hbm, hbm, hbm, pl.BlockSpec(memory_space=pltpu.VMEM)],
-            out_specs=[hbm, hbm],
+            out_specs=[pl.BlockSpec(memory_space=pltpu.VMEM)] * 2,
             scratch_shapes=[
                 pltpu.VMEM((4, group, n_kg, 2, 8, 128), F32),
                 pltpu.VMEM((n_kg, 2, 2, group, 2, 8, 128), F32),
@@ -283,9 +279,7 @@
                 pltpu.VMEM((RING, n_deg, lat_rows), F32),
                 pltpu.VMEM((RING, 2, levels, n_deg), F32),
                 pltpu.VMEM(dft.shape, BF16),
-                pltpu.VMEM((2, 8, lat_loc, 2 * wave_num), F32),
-                pltpu.VMEM((2, 2, levels, n_deg), F32),
-                dma((RING,)), dma((RING,)), dma, dma((2,)), dma((2,)), dma((4,)), dma((4,)), dma((3 + levels // 8,)), dma((4,)),
+                dma((RING,)), dma((RING,)), dma, dma((4,)), dma((4,)), dma((3 + levels // 8,)), dma((4,)),
             ],
             compiler_params=pltpu.CompilerParams(vmem_limit_bytes=VMEM_LIMIT, collective_id=0, has_side_effects=True),
             name='transform_pair',

time: 305 us -> 299 us (0.980)
  local copies, waits for them, and re-layouts: 10.9 us -> 5.41 us
    unnamed x4 -> x2, local copies, waits for them, and re-layouts: 9.47 us -> 5.41 us
where the time goes in v3:
time: 299 us; the launch traced here: 295 us
  Pallas kernels  288 us (96%)
  local copies, waits for them, and re-layouts  5.41 us (2%)
    pallas_call x1, Pallas kernels, per_device(): pl.pallas_call(functools.partial(whole_kernel, group), out_shape=[pltpu.V...  288 us

profile of v3, /device:TPU:15, one launch (start us, length us, event | category | flops | bytes accessed | tf_op | source)
XLA Modules:
  0.0 294.5 jit_solution(18256173375007976977)
XLA Ops:
  0.6 288.5 %transform_pair.1 = (f32[48,32,1024]{2,1,0:T(8,128)S(1)}, f32[32,2,48,512]{3,2,1,0:T(8,128)S(1)}) custom-call(f32[32,2,48,512]{3,2,1,0:T(8,128)} %coef.1, f32[512,512,512]{2,1,0:T(8,128)} %leg.1, bf16[2,2,512,512]{3,2,1,0:T(8,128)(2,1)} %constant.2.clone.dft_hbm, f32[4,128]{1,0:T(4,128)} %bitcast.1), custom_call_target="tpu_custom_call" | custom-call | tf_op jit(solution)/shard_map/transform_pair/pallas_call | solution.py:268
  289.1 2.7 copy.8
  291.8 2.7 copy.9
